TPU v7x, 32 devices: a whole 2x2x4 slice. The times are simulated.
32 devices in a mesh: obs: 8 (over z, y), chan: 4 (over x, core).
Axes of the slice: x: 2, y: 2, z: 4, core: 2. Of those that a mesh axis runs over, the one named last changes fastest.
Arguments:
- jacobian: bfloat16 [2048, 128, 137], P('obs', 'chan'), may hold values from -0.5 to 0.5
- departures: float32 [128, 2048], P('chan', 'obs'), may hold values from -6 to 6
- obs_weights: float32 [128, 2048], P('chan', 'obs'), may hold values from 0.25 to 4
- column_count: int32 [8], P('obs'), may hold values from 1 to 256, as said below
- grid_block: int32 [16], P('obs'), may hold values from 0 to 15, as said below
- sqrt_cov: float32 [137, 137], replicated, may hold values from -0.5 to 0.5
Outputs:
- increment: float32 [2048, 137], P('obs')
- residual: float32 [2048, 137], P('obs')
Inputs may be any that keep to these rules, and one draw needn't show every extreme that they name: The first column_count of a device's 256 column slots are observed; some device has all 256 observed in every draw. `grid_block`: the owner of grid block g is index g // 2 of obs. The 2 blocks of one device match blocks of 2 different owners; in every draw some owner has a block matched by each device (every device matches one of that owner's blocks), and some device matches that owner's last block.
All inputs are finite; a program needn't handle non-finite values.
Results may differ from a plain program's by a relative error of at most 0.02.
Values may be sent and summed in bfloat16 or wider, within the bound.
A program may use at most 64 MiB of HBM per device.

v0:
```python
import jax
import jax.numpy as jnp
from jax import lax
from jax.sharding import PartitionSpec as P

BLOCK = 128
ITERS = 5
GRID_BLK = 2


def block_terms(jac_part, weight_part, mask_part, predicted):
    scaled = (mask_part[:, None] * weight_part * predicted).astype(jnp.bfloat16)
    return lax.dot_general(
        jac_part, scaled, (((1,), (1,)), ((0,), (0,))), preferred_element_type=jnp.float32
    )


def forward_terms(jac_part, weight_part, mask_part, field_part):
    predicted = lax.dot_general(
        jac_part, field_part, (((2,), (1,)), ((0,), (0,))), preferred_element_type=jnp.float32
    )
    return block_terms(jac_part, weight_part, mask_part, predicted)


def per_device(jacobian, departures, obs_weights, column_count, grid_block, sqrt_cov):
    obs_count = lax.axis_size("obs")
    myself = lax.axis_index("obs")
    capacity, group_channels, layers = jacobian.shape
    block_count = capacity // BLOCK
    weight_cols = obs_weights.T
    depart_cols = departures.T
    observed = (jnp.arange(capacity, dtype=jnp.int32) < column_count[0]).astype(jnp.float32)
    every_id = lax.all_gather(grid_block, "obs", axis=0, tiled=True).reshape(obs_count, block_count)
    targets = jnp.arange(obs_count, dtype=jnp.int32)
    send_pick = (grid_block[None, :] // GRID_BLK == targets[:, None]).astype(jnp.float32)
    owned_here = every_id // GRID_BLK == myself
    places = every_id % GRID_BLK
    grid_index = jnp.arange(GRID_BLK, dtype=jnp.int32)
    take_pick = jnp.sum(
        ((places[None] == grid_index[:, None, None]) & owned_here[None]).astype(jnp.float32), axis=2
    )
    share_cols = BLOCK

    def local_terms(kernel_fn, inputs):
        return kernel_fn(jacobian, weight_cols, observed, inputs)

    def to_owners(terms):
        blocked = terms.reshape(block_count, BLOCK, layers)
        blocked = lax.psum(blocked, "chan")
        outgoing = jnp.dot(
            send_pick, blocked.reshape(block_count, -1), precision=lax.Precision.HIGHEST
        )
        incoming = lax.all_to_all(
            outgoing.reshape(obs_count, share_cols, layers),
            "obs",
            split_axis=0,
            concat_axis=0,
            tiled=True,
        )
        summed = jnp.dot(
            take_pick, incoming.reshape(obs_count, -1), precision=lax.Precision.HIGHEST
        )
        return summed.reshape(GRID_BLK, share_cols, layers)

    def spread(field):
        return jnp.dot(
            field.reshape(-1, layers), sqrt_cov, precision=lax.Precision.HIGHEST
        ).reshape(field.shape)

    def spread_back(field):
        flat = lax.dot_general(
            field.reshape(-1, layers),
            sqrt_cov,
            (((1,), (1,)), ((), ())),
            precision=lax.Precision.HIGHEST,
        )
        return flat.reshape(field.shape)

    def squared(values):
        partial_sum = jnp.sum(values * values)
        return lax.psum(partial_sum, "obs")

    residual = spread_back(to_owners(local_terms(block_terms, depart_cols)))
    control = jnp.zeros_like(residual)
    direction = residual
    norm_now = squared(residual)
    for iteration in range(ITERS):
        rounded = spread(direction).astype(jnp.bfloat16).reshape(GRID_BLK, -1)
        to_outgoing = jnp.dot(
            take_pick.T.astype(jnp.bfloat16), rounded, preferred_element_type=jnp.float32
        ).astype(jnp.bfloat16)
        to_incoming = lax.all_to_all(
            to_outgoing.reshape(obs_count, share_cols, layers),
            "obs",
            split_axis=0,
            concat_axis=0,
            tiled=True,
        )
        picked = jnp.dot(
            send_pick.T.astype(jnp.bfloat16),
            to_incoming.reshape(obs_count, -1),
            preferred_element_type=jnp.float32,
        )
        picked = picked.astype(jnp.bfloat16).reshape(block_count, share_cols, layers)
        fetched = picked.reshape(capacity, layers)
        image = direction + spread_back(to_owners(local_terms(forward_terms, fetched)))
        curvature_partial_sum = jnp.sum(direction * image)
        step_length = norm_now / lax.psum(curvature_partial_sum, "obs")
        control = control + step_length * direction
        residual = residual - step_length * image
        norm_next = squared(residual)
        direction = residual + norm_next / norm_now * direction
        norm_now = norm_next
    increment = spread(control)
    return (increment.reshape(-1, layers), residual.reshape(-1, layers))


def solution(mesh):
    in_specs = (P("obs", "chan", None), P("chan", "obs"), P("chan", "obs"), P("obs"), P("obs"), P())
    out_specs = (P("obs", None), P("obs", None))
    return jax.shard_map(
        per_device, mesh=mesh, in_specs=in_specs, out_specs=out_specs, check_vma=False
    )
```

profile of v0, /device:TPU:0, one launch (start us, length us, event | category | flops | bytes accessed | tf_op | source)
XLA Modules:
  0.0 699.7 jit_solution(8581663738396648842)
XLA Ops:
  8.7 2.5 fusion.5
  13.1 33.3 %all-reduce.9.cloned.1.call-done = f32[128,137,2]{0,2,1:T(2,128)} async-done(((f32[128,137,2]{0,2,1:T(2,128)}), f32[128,137,2]{0,2,1:T(2,128)}) %all-reduce.9.cloned.1.call-update) | async-done | bytes 140304 | tf_op jit(solution)/shard_map/psum | solution.py:49
  48.7 5.5 all-to-all-start
  55.7 14.9 %all-reduce = s32[16]{0:T(128)S(1)} all-reduce(s32[16]{0:T(128)S(1)} %dynamic-update-slice), channel_id=1, replica_groups=mesh['obs'=8,'chan'=4] {'obs'}, use_global_device_ids=true, to_apply=%add | all-reduce | flops 16 | bytes 128
  77.3 14.5 %all_to_all.55 = bf16[8,128,137]{1,2,0:T(8,128)(2,1)} all-to-all(bf16[8,128,137]{1,2,0:T(8,128)(2,1)} %copy.105), channel_id=1, replica_groups=mesh['obs'=8,'chan'=4] {'obs'}, dimensions={0} | all-to-all | bytes 561152 | tf_op jit(solution)/shard_map/all_to_all | solution.py:92
  99.4 27.9 %all-reduce.11.cloned.1.call-done = f32[128,137,2]{0,2,1:T(2,128)} async-done(((f32[128,137,2]{0,2,1:T(2,128)}), f32[128,137,2]{0,2,1:T(2,128)}) %all-reduce.11.cloned.1.call-update) | async-done | bytes 140304 | tf_op jit(solution)/shard_map/psum | solution.py:49
  129.7 5.5 all-to-all-start.2
  135.3 16.2 %all-to-all-done.2 = f32[8,128,137]{1,2,0:T(8,128)S(1)} async-done(((f32[8,128,137]{1,2,0:T(8,128)}), f32[8,128,137]{1,2,0:T(8,128)S(1)}, u32[]{:S(2)}, u32[]{:S(2)}) %all-to-all-start.2) | async-done | bytes 561184 | tf_op jit(solution)/shard_map/all_to_all | solution.py:53
  152.8 1.7 reshape.247
  154.5 2.2 dot_general.194
  156.7 1.6 copy.110
  159.8 20.1 %all-reduce.1 = (f32[]{:T(128)}, f32[]{:T(128)}) all-reduce(f32[]{:T(128)} %get-tuple-element.10, f32[]{:T(128)} %get-tuple-element.12), channel_id=1, replica_groups=mesh['obs'=8,'chan'=4] {'obs'}, use_global_device_ids=true, to_apply=%region_3.4 | all-reduce | flops 2 | bytes 16 | tf_op jit(solution)/shard_map/psum | solution.py:81
  181.9 17.7 %psum.116 = f32[]{:T(128)} all-reduce(f32[]{:T(128)} %multiply_reduce_fusion.7), channel_id=1, replica_groups=mesh['obs'=8,'chan'=4] {'obs'}, use_global_device_ids=true, to_apply=%region_8.9 | all-reduce | flops 1 | bytes 8 | tf_op jit(solution)/shard_map/psum | solution.py:81
  202.9 2.3 reshape.249
  206.1 13.2 %all_to_all.56 = bf16[8,128,137]{1,2,0:T(8,128)(2,1)} all-to-all(bf16[8,128,137]{1,2,0:T(8,128)(2,1)} %copy.119), channel_id=1, replica_groups=mesh['obs'=8,'chan'=4] {'obs'}, dimensions={0} | all-to-all | bytes 561152 | tf_op jit(solution)/shard_map/all_to_all | solution.py:92
  227.0 27.8 %all-reduce.13.cloned.1.call-done = f32[128,137,2]{0,2,1:T(2,128)} async-done(((f32[128,137,2]{0,2,1:T(2,128)}), f32[128,137,2]{0,2,1:T(2,128)}) %all-reduce.13.cloned.1.call-update) | async-done | bytes 140304 | tf_op jit(solution)/shard_map/psum | solution.py:49
  256.4 22.2 %all_to_all.57 = f32[8,128,137]{1,2,0:T(8,128)S(1)} all-to-all(f32[8,128,137]{1,2,0:T(8,128)S(1)} %copy.122), channel_id=1, replica_groups=mesh['obs'=8,'chan'=4] {'obs'}, dimensions={0} | all-to-all | bytes 1122304 | tf_op jit(solution)/shard_map/all_to_all | solution.py:53
  279.9 1.7 reshape.253
  281.6 2.2 dot_general.206
  283.8 1.6 copy.124
  286.9 19.5 %psum.118 = f32[]{:T(128)} all-reduce(f32[]{:T(128)} %get-tuple-element.14), channel_id=1, replica_groups=mesh['obs'=8,'chan'=4] {'obs'}, use_global_device_ids=true, to_apply=%region_11.12 | all-reduce | flops 1 | bytes 8 | tf_op jit(solution)/shard_map/psum | solution.py:108
  308.3 18.1 %psum.119 = f32[]{:T(128)} all-reduce(f32[]{:T(128)} %get-tuple-element.8), channel_id=1, replica_groups=mesh['obs'=8,'chan'=4] {'obs'}, use_global_device_ids=true, to_apply=%region_13.14 | all-reduce | flops 1 | bytes 8 | tf_op jit(solution)/shard_map/psum | solution.py:81
  329.7 2.3 reshape.255
  332.9 13.0 %all_to_all.58 = bf16[8,128,137]{1,2,0:T(8,128)(2,1)} all-to-all(bf16[8,128,137]{1,2,0:T(8,128)(2,1)} %copy.128), channel_id=1, replica_groups=mesh['obs'=8,'chan'=4] {'obs'}, dimensions={0} | all-to-all | bytes 561152 | tf_op jit(solution)/shard_map/all_to_all | solution.py:92
  353.5 27.8 %all-reduce.15.cloned.1.call-done = f32[128,137,2]{0,2,1:T(2,128)} async-done(((f32[128,137,2]{0,2,1:T(2,128)}), f32[128,137,2]{0,2,1:T(2,128)}) %all-reduce.15.cloned.1.call-update) | async-done | bytes 140304 | tf_op jit(solution)/shard_map/psum | solution.py:49
  382.8 22.2 %all_to_all.59 = f32[8,128,137]{1,2,0:T(8,128)S(1)} all-to-all(f32[8,128,137]{1,2,0:T(8,128)S(1)} %copy.131), channel_id=1, replica_groups=mesh['obs'=8,'chan'=4] {'obs'}, dimensions={0} | all-to-all | bytes 1122304 | tf_op jit(solution)/shard_map/all_to_all | solution.py:53
  406.4 1.7 reshape.259
  408.1 2.2 dot_general.218
  413.4 19.5 %psum.121 = f32[]{:T(128)} all-reduce(f32[]{:T(128)} %get-tuple-element.16), channel_id=1, replica_groups=mesh['obs'=8,'chan'=4] {'obs'}, use_global_device_ids=true, to_apply=%region_16.17 | all-reduce | flops 1 | bytes 8 | tf_op jit(solution)/shard_map/psum | solution.py:108
  434.9 18.1 %psum.122 = f32[]{:T(128)} all-reduce(f32[]{:T(128)} %get-tuple-element.6), channel_id=1, replica_groups=mesh['obs'=8,'chan'=4] {'obs'}, use_global_device_ids=true, to_apply=%region_18.19 | all-reduce | flops 1 | bytes 8 | tf_op jit(solution)/shard_map/psum | solution.py:81
  456.3 2.3 reshape.261
  459.5 13.1 %all_to_all.60 = bf16[8,128,137]{1,2,0:T(8,128)(2,1)} all-to-all(bf16[8,128,137]{1,2,0:T(8,128)(2,1)} %copy.137), channel_id=1, replica_groups=mesh['obs'=8,'chan'=4] {'obs'}, dimensions={0} | all-to-all | bytes 561152 | tf_op jit(solution)/shard_map/all_to_all | solution.py:92
  480.2 27.8 %all-reduce.17.cloned.1.call-done = f32[128,137,2]{0,2,1:T(2,128)} async-done(((f32[128,137,2]{0,2,1:T(2,128)}), f32[128,137,2]{0,2,1:T(2,128)}) %all-reduce.17.cloned.1.call-update) | async-done | bytes 140304 | tf_op jit(solution)/shard_map/psum | solution.py:49
  509.6 22.3 %all_to_all.61 = f32[8,128,137]{1,2,0:T(8,128)} all-to-all(f32[8,128,137]{1,2,0:T(8,128)S(1)} %copy.140), channel_id=1, replica_groups=mesh['obs'=8,'chan'=4] {'obs'}, dimensions={0} | all-to-all | bytes 1122304 | tf_op jit(solution)/shard_map/all_to_all | solution.py:53
  531.9 2.4 copy.141
  534.3 1.7 reshape.265
  536.0 2.2 dot_general.230
  538.2 1.6 copy.142
  541.3 19.5 %psum.124 = f32[]{:T(128)} all-reduce(f32[]{:T(128)} %get-tuple-element.18), channel_id=1, replica_groups=mesh['obs'=8,'chan'=4] {'obs'}, use_global_device_ids=true, to_apply=%region_21.22 | all-reduce | flops 1 | bytes 8 | tf_op jit(solution)/shard_map/psum | solution.py:108
  563.6 18.0 %psum.125 = f32[]{:T(128)} all-reduce(f32[]{:T(128)} %get-tuple-element.4), channel_id=1, replica_groups=mesh['obs'=8,'chan'=4] {'obs'}, use_global_device_ids=true, to_apply=%region_23.24 | all-reduce | flops 1 | bytes 8 | tf_op jit(solution)/shard_map/psum | solution.py:81
  585.8 2.0 reshape.267
  587.8 2.0 copy.146
  589.8 13.1 %all_to_all.62 = bf16[8,128,137]{1,2,0:T(8,128)(2,1)} all-to-all(bf16[8,128,137]{1,2,0:T(8,128)(2,1)} %copy.146), channel_id=1, replica_groups=mesh['obs'=8,'chan'=4] {'obs'}, dimensions={0} | all-to-all | bytes 561152 | tf_op jit(solution)/shard_map/all_to_all | solution.py:92
  602.9 2.0 copy.147
  604.8 2.4 reshape.268
  613.9 27.8 %all-reduce.19.cloned.1.call-done = f32[128,137,2]{0,2,1:T(2,128)} async-done(((f32[128,137,2]{0,2,1:T(2,128)}), f32[128,137,2]{0,2,1:T(2,128)}) %all-reduce.19.cloned.1.call-update) | async-done | bytes 140304 | tf_op jit(solution)/shard_map/psum | solution.py:49
  643.3 22.2 %all_to_all.63 = f32[8,128,137]{1,2,0:T(8,128)S(1)} all-to-all(f32[8,128,137]{1,2,0:T(8,128)S(1)} %copy.149), channel_id=1, replica_groups=mesh['obs'=8,'chan'=4] {'obs'}, dimensions={0} | all-to-all | bytes 1122304 | tf_op jit(solution)/shard_map/all_to_all | solution.py:53
  669.4 19.5 %psum.127 = f32[]{:T(128)} all-reduce(f32[]{:T(128)} %get-tuple-element.20), channel_id=1, replica_groups=mesh['obs'=8,'chan'=4] {'obs'}, use_global_device_ids=true, to_apply=%region_26.27 | all-reduce | flops 1 | bytes 8 | tf_op jit(solution)/shard_map/psum | solution.py:108
  (207 shorter events, 90.3 us)
Async XLA Ops:
  7.2 65.6 %copy-start = (f32[137,137]{1,0:T(8,128)S(1)}, f32[137,137]{1,0:T(8,128)}, u32[]{:S(2)}) copy-start(f32[137,137]{1,0:T(8,128)} %param.11) | copy-start | bytes 225232
  7.2 5.8 copy-start.19
  7.2 39.1 %all-reduce.9.cloned.1.call-start = ((), (), s32[]{:S(2)}) async-start(), calls=%async_computation.11 | async-start | bytes 280576 | tf_op jit(solution)/shard_map/psum | solution.py:49
  7.9 88.8 %copy-start.14 = (f32[256]{0:T(256)}, f32[256]{0:T(256)S(1)}, u32[]{:S(2)}) copy-start(f32[256]{0:T(256)S(1)} %compare_convert_fusion.1) | copy-start | bytes 3076
  11.4 42.9 %copy-start.20 = (u32[32]{0:T(128)S(1)}, u32[32]{0:T(128)}, u32[]{:S(2)}) copy-start(u32[32]{0:T(128)} %constant.47) | copy-start | bytes 388
  13.0 114.3 %copy-start.8 = (s32[2]{0:T(128)}, s32[2]{0:T(128)S(1)}, u32[]{:S(2)}) copy-start(s32[2]{0:T(128)S(1)} %and_select_fusion) | copy-start | bytes 28
  48.7 22.3 %all-to-all-start = ((f32[8,128,137]{1,2,0:T(8,128)}), f32[8,128,137]{1,2,0:T(8,128)S(1)}, u32[]{:S(2)}, u32[]{:S(2)}) async-start(f32[8,128,137]{1,2,0:T(8,128)} %copy.102), calls=%async_computation | async-start | bytes 1179648 | tf_op jit(solution)/shard_map/all_to_all | solution.py:53
  54.2 73.1 %all-reduce.11.cloned.1.call-start = ((), (), s32[]{:S(2)}) async-start(), calls=%async_computation.12 | async-start | bytes 280576 | tf_op jit(solution)/shard_map/psum | solution.py:49
  71.0 0.9 copy-start.11
  71.0 3.8 copy-start.17
  75.1 20.9 %copy-start.1 = (bf16[256,32,137]{0,1,2:T(8,128)(2,1)S(1)}, bf16[256,32,137]{0,1,2:T(8,128)(2,1)}, u32[]{:S(2)}) copy-start(bf16[256,32,137]{0,1,2:T(8,128)(2,1)} %param.6) | copy-start | bytes 6733828
  91.8 5.0 copy-start.5
  129.7 21.8 %all-to-all-start.2 = ((f32[8,128,137]{1,2,0:T(8,128)}), f32[8,128,137]{1,2,0:T(8,128)S(1)}, u32[]{:S(2)}, u32[]{:S(2)}) async-start(f32[8,128,137]{1,2,0:T(8,128)} %copy.108), calls=%async_computation.2 | async-start | bytes 1179648 | tf_op jit(solution)/shard_map/all_to_all | solution.py:53
  135.2 119.6 %all-reduce.13.cloned.1.call-start = ((), (), s32[]{:S(2)}) async-start(), calls=%async_computation.13 | async-start | bytes 280576 | tf_op jit(solution)/shard_map/psum | solution.py:49
  152.8 5.5 copy-start.12
  156.7 45.2 %copy-start.18 = (bf16[2,8]{1,0:T(2,128)(2,1)S(1)}, bf16[2,8]{1,0:T(2,128)(2,1)}, u32[]{:S(2)}) copy-start(bf16[2,8]{1,0:T(2,128)(2,1)} %copy-done.17) | copy-start | bytes 100
  201.5 20.3 %copy-start.9 = (s32[2]{0:T(128)S(1)}, s32[2]{0:T(128)}, u32[]{:S(2)}) copy-start(s32[2]{0:T(128)} %copy-done.8) | copy-start | bytes 28
  219.3 4.9 copy-start.15
  227.0 154.3 %all-reduce.15.cloned.1.call-start = ((), (), s32[]{:S(2)}) async-start(), calls=%async_computation.14 | async-start | bytes 280576 | tf_op jit(solution)/shard_map/psum | solution.py:49
  308.3 20.4 %copy-start.3 = (f32[2,128,137]{1,2,0:T(8,128)}, f32[2,128,137]{1,2,0:T(8,128)S(1)}, u32[]{:S(2)}) copy-start(f32[2,128,137]{1,2,0:T(8,128)S(1)} %get-tuple-element.9) | copy-start | bytes 420868
  353.5 154.6 %all-reduce.17.cloned.1.call-start = ((), (), s32[]{:S(2)}) async-start(), calls=%async_computation.15 | async-start | bytes 280576 | tf_op jit(solution)/shard_map/psum | solution.py:49
  408.1 26.1 %copy-start.4 = (f32[2,128,137]{1,2,0:T(8,128)S(1)}, f32[2,128,137]{1,2,0:T(8,128)}, u32[]{:S(2)}) copy-start(f32[2,128,137]{1,2,0:T(8,128)} %copy-done.3) | copy-start | bytes 420868
  434.9 20.4 %copy-start.2 = (f32[2,128,137]{1,2,0:T(8,128)}, f32[2,128,137]{1,2,0:T(8,128)S(1)}, u32[]{:S(2)}) copy-start(f32[2,128,137]{1,2,0:T(8,128)S(1)} %get-tuple-element.7) | copy-start | bytes 420868
  472.6 4.9 copy-start.6
  480.2 161.6 %all-reduce.19.cloned.1.call-start = ((), (), s32[]{:S(2)}) async-start(), calls=%async_computation.16 | async-start | bytes 280576 | tf_op jit(solution)/shard_map/psum | solution.py:49
  602.9 8.4 %copy-start.7 = (f32[32,256]{1,0:T(8,128)S(1)}, f32[32,256]{1,0:T(8,128)}, u32[]{:S(2)}) copy-start(f32[32,256]{1,0:T(8,128)} %param.8) | copy-start | bytes 98308
  602.9 8.4 %copy-start.16 = (f32[256]{0:T(256)S(1)}, f32[256]{0:T(256)}, u32[]{:S(2)}) copy-start(f32[256]{0:T(256)} %copy-done.14) | copy-start | bytes 3076
  611.2 30.5 %copy-start.10 = (s32[2]{0:T(128)S(1)}, s32[2]{0:T(128)}, u32[]{:S(2)}) copy-start(s32[2]{0:T(128)} %copy-done.8) | copy-start | bytes 28
  665.9 2.1 copy-start.13
Sparse Core Ops, SparseCore 0:
  13.1 33.1 all-reduce.8
  99.5 27.7 all-reduce.10
  227.1 27.6 all-reduce.12
  353.6 27.6 all-reduce.14
  480.3 27.6 all-reduce.16
  614.0 27.6 all-reduce.18
where the time goes:
time: 708 us; the launch traced here: 700 us
  blocking collectives  341 us (48%)
  waiting for transfers between devices  189 us (27%)
  local copies, waits for them, and re-layouts  83.4 us (12%)
  matrix products  31.8 us (4%)
  between operations  28.7 us (4%)
  other arithmetic  15.2 us (2%)
  starting transfers between devices  11.3 us (2%)
    psum x6, waiting for transfers between devices, to_owners(): blocked = lax.psum(blocked, 'chan')  172 us
    psum x5, blocking collectives, squared(): return lax.psum(partial_sum, 'obs')  92.1 us
    all_to_all x4, blocking collectives, to_owners(): lax.all_to_all(outgoing.reshape(obs_count, share_cols, layers), 'obs', sp...  89 us
    psum x4, blocking collectives, per_device(): step_length = norm_now / lax.psum(curvature_partial_sum, 'obs')  77.8 us
    all_to_all x5, blocking collectives, per_device(): lax.all_to_all(to_outgoing.reshape(obs_count, share_cols, layers), 'obs',...  66.9 us
    dot_general x10, local copies, waits for them, and re-layouts, to_owners(): jnp.dot(take_pick, incoming.reshape(obs_count, -1), precision=lax.Precisi...  16.5 us
    all_to_all x2, waiting for transfers between devices, to_owners(): lax.all_to_all(outgoing.reshape(obs_count, share_cols, layers), 'obs', sp...  16.2 us
    reshape x10, local copies, waits for them, and re-layouts, per_device(): to_outgoing.reshape(obs_count, share_cols, layers)  15.7 us
  transfers between devices with their start and end apart: 8, of which 7 were waited for; matrix products, arithmetic and copies ran while one was open for 0% of the time, Pallas kernels for 0%

commit v1 on v0

--- a/solution.py
+++ b/solution.py
@@ -46,7 +46,7 @@
 
     def to_owners(terms):
         blocked = terms.reshape(block_count, BLOCK, layers)
-        blocked = lax.psum(blocked, "chan")
+        blocked = jnp.sum(lax.all_gather(blocked, "chan"), axis=0)
         outgoing = jnp.dot(
             send_pick, blocked.reshape(block_count, -1), precision=lax.Precision.HIGHEST
         )

time: 708 us -> 557 us (0.79)
  waiting for transfers between devices: 189 us -> 16.6 us
  blocking collectives: 341 us -> 375 us
  between operations: 28.7 us -> 15.6 us
    psum x6 -> x0, waiting for transfers between devices: 172 us -> none  [to_owners(): blocked = lax.psum(blocked, 'chan')]
    all_gather x0 -> x6, blocking collectives: none -> 45 us  [to_owners(): blocked = jnp.sum(lax.all_gather(blocked, 'chan'), axis=0)]
    all_to_all x4, blocking collectives: 89 us -> 79.5 us  [to_owners(): lax.all_to_all(outgoing.reshape(obs_count, share_cols, layers), 'obs', sp...]
    unnamed x12 -> x6, other arithmetic: 7.93 us -> 0.83 us
    dot_general x0 -> x6, other arithmetic: none -> 7.1 us  [block_terms(): lax.dot_general(jac_part, scaled, (((1,), (1,)), ((0,), (0,))), preferred...]
  transfers between devices with their start and end apart: 8 -> 2, of which waited for: 7 -> 1; matrix products, arithmetic and copies ran while one was open for 0% -> 0% of each run, Pallas kernels for 0% -> 0%
where the time goes in v1:
time: 557 us; the launch traced here: 547 us
  blocking collectives  375 us (67%)
  local copies, waits for them, and re-layouts  83.8 us (15%)
  matrix products  27.3 us (5%)
  other arithmetic  18.8 us (3%)
  waiting for transfers between devices  16.6 us (3%)
  between operations  15.6 us (3%)
  starting transfers between devices  9.37 us (2%)
    psum x5, blocking collectives, squared(): return lax.psum(partial_sum, 'obs')  92.1 us
    all_to_all x4, blocking collectives, to_owners(): lax.all_to_all(outgoing.reshape(obs_count, share_cols, layers), 'obs', sp...  79.5 us
    psum x4, blocking collectives, per_device(): step_length = norm_now / lax.psum(curvature_partial_sum, 'obs')  77.8 us
    all_to_all x5, blocking collectives, per_device(): lax.all_to_all(to_outgoing.reshape(obs_count, share_cols, layers), 'obs',...  65.6 us
    all_gather x6, blocking collectives, to_owners(): blocked = jnp.sum(lax.all_gather(blocked, 'chan'), axis=0)  45 us
    all_to_all x2, waiting for transfers between devices, to_owners(): lax.all_to_all(outgoing.reshape(obs_count, share_cols, layers), 'obs', sp...  16.6 us
    dot_general x10, local copies, waits for them, and re-layouts, to_owners(): jnp.dot(take_pick, incoming.reshape(obs_count, -1), precision=lax.Precisi...  16.5 us
    reshape x10, local copies, waits for them, and re-layouts, per_device(): to_outgoing.reshape(obs_count, share_cols, layers)  15.7 us
  transfers between devices with their start and end apart: 2, of which 1 were waited for; matrix products, arithmetic and copies ran while one was open for 0% of the time, Pallas kernels for 0%

profile of v1, /device:TPU:0, one launch (start us, length us, event | category | flops | bytes accessed | tf_op | source)
XLA Modules:
  0.0 546.5 jit_solution(2209927683074864746)
XLA Ops:
  2.8 2.5 fusion.5
  5.4 8.8 %all_gather.22 = f32[4,2,128,137]{2,1,3,0:T(2,128)S(1)} all-gather(f32[1,2,128,137]{2,1,3,0:T(2,128)S(1)} %all_gather_reshape.18), channel_id=1, replica_groups=mesh['obs'=8,'chan'=4] {'chan'}, dimensions={0}, use_global_device_ids=true | all-gather | bytes 701440 | tf_op jit(solution)/shard_map/all_gather | solution.py:49
  17.1 5.8 %all-to-all-start = ((f32[8,128,137]{1,2,0:T(8,128)}), f32[8,128,137]{1,2,0:T(8,128)S(1)}, u32[]{:S(2)}, u32[]{:S(2)}) async-start(f32[8,128,137]{1,2,0:T(8,128)} %copy.163), calls=%async_computation | async-start | bytes 1179648 | tf_op jit(solution)/shard_map/all_to_all | solution.py:53
  24.4 15.1 %all-reduce = s32[16]{0:T(128)S(1)} all-reduce(s32[16]{0:T(128)S(1)} %dynamic-update-slice), channel_id=1, replica_groups=mesh['obs'=8,'chan'=4] {'obs'}, use_global_device_ids=true, to_apply=%add | all-reduce | flops 16 | bytes 128
  46.1 14.3 %all_to_all.55 = bf16[8,128,137]{1,2,0:T(8,128)(2,1)} all-to-all(bf16[8,128,137]{1,2,0:T(8,128)(2,1)} %copy.166), channel_id=1, replica_groups=mesh['obs'=8,'chan'=4] {'obs'}, dimensions={0} | all-to-all | bytes 561152 | tf_op jit(solution)/shard_map/all_to_all | solution.py:92
  66.4 7.2 %all_gather.23 = f32[4,2,128,137]{2,1,3,0:T(2,128)S(1)} all-gather(f32[1,2,128,137]{2,1,3,0:T(2,128)S(1)} %all_gather_reshape.19), channel_id=1, replica_groups=mesh['obs'=8,'chan'=4] {'chan'}, dimensions={0}, use_global_device_ids=true | all-gather | bytes 701440 | tf_op jit(solution)/shard_map/all_gather | solution.py:49
  76.4 3.5 all-to-all-start.2
  80.0 16.6 %all-to-all-done.2 = f32[8,128,137]{1,2,0:T(8,128)S(1)} async-done(((f32[8,128,137]{1,2,0:T(8,128)}), f32[8,128,137]{1,2,0:T(8,128)S(1)}, u32[]{:S(2)}, u32[]{:S(2)}) %all-to-all-start.2) | async-done | bytes 561184 | tf_op jit(solution)/shard_map/all_to_all | solution.py:53
  97.9 1.7 reshape.227
  99.6 2.2 dot_general.194
  101.8 1.6 copy.172
  104.9 20.1 %all-reduce.1 = (f32[]{:T(128)}, f32[]{:T(128)}) all-reduce(f32[]{:T(128)} %get-tuple-element.10, f32[]{:T(128)} %get-tuple-element.12), channel_id=1, replica_groups=mesh['obs'=8,'chan'=4] {'obs'}, use_global_device_ids=true, to_apply=%region_3.4 | all-reduce | flops 2 | bytes 16 | tf_op jit(solution)/shard_map/psum | solution.py:81
  126.9 17.7 %psum.72 = f32[]{:T(128)} all-reduce(f32[]{:T(128)} %multiply_reduce_fusion.7), channel_id=1, replica_groups=mesh['obs'=8,'chan'=4] {'obs'}, use_global_device_ids=true, to_apply=%region_8.9 | all-reduce | flops 1 | bytes 8 | tf_op jit(solution)/shard_map/psum | solution.py:81
  148.1 2.3 reshape.229
  151.2 12.8 %all_to_all.56 = bf16[8,128,137]{1,2,0:T(8,128)(2,1)} all-to-all(bf16[8,128,137]{1,2,0:T(8,128)(2,1)} %copy.181), channel_id=1, replica_groups=mesh['obs'=8,'chan'=4] {'obs'}, dimensions={0} | all-to-all | bytes 561152 | tf_op jit(solution)/shard_map/all_to_all | solution.py:92
  170.7 7.4 %all_gather.24 = f32[4,2,128,137]{2,1,3,0:T(2,128)S(1)} all-gather(f32[1,2,128,137]{2,1,3,0:T(2,128)} %all_gather_reshape.20), channel_id=1, replica_groups=mesh['obs'=8,'chan'=4] {'chan'}, dimensions={0}, use_global_device_ids=true | all-gather | bytes 701440 | tf_op jit(solution)/shard_map/all_gather | solution.py:49
  183.2 19.7 %all_to_all.57 = f32[8,128,137]{1,2,0:T(8,128)S(1)} all-to-all(f32[8,128,137]{1,2,0:T(8,128)S(1)} %copy.185), channel_id=1, replica_groups=mesh['obs'=8,'chan'=4] {'obs'}, dimensions={0} | all-to-all | bytes 1122304 | tf_op jit(solution)/shard_map/all_to_all | solution.py:53
  204.3 1.7 reshape.232
  206.0 2.2 dot_general.206
  208.1 1.6 copy.187
  211.2 19.4 %psum.73 = f32[]{:T(128)} all-reduce(f32[]{:T(128)} %get-tuple-element.14), channel_id=1, replica_groups=mesh['obs'=8,'chan'=4] {'obs'}, use_global_device_ids=true, to_apply=%region_11.12 | all-reduce | flops 1 | bytes 8 | tf_op jit(solution)/shard_map/psum | solution.py:108
  232.7 18.1 %psum.74 = f32[]{:T(128)} all-reduce(f32[]{:T(128)} %get-tuple-element.8), channel_id=1, replica_groups=mesh['obs'=8,'chan'=4] {'obs'}, use_global_device_ids=true, to_apply=%region_13.14 | all-reduce | flops 1 | bytes 8 | tf_op jit(solution)/shard_map/psum | solution.py:81
  254.2 2.3 reshape.234
  257.4 12.8 %all_to_all.58 = bf16[8,128,137]{1,2,0:T(8,128)(2,1)} all-to-all(bf16[8,128,137]{1,2,0:T(8,128)(2,1)} %copy.191), channel_id=1, replica_groups=mesh['obs'=8,'chan'=4] {'obs'}, dimensions={0} | all-to-all | bytes 561152 | tf_op jit(solution)/shard_map/all_to_all | solution.py:92
  276.1 7.1 %all_gather.25 = f32[4,2,128,137]{2,1,3,0:T(2,128)S(1)} all-gather(f32[1,2,128,137]{2,1,3,0:T(2,128)S(1)} %all_gather_reshape.21), channel_id=1, replica_groups=mesh['obs'=8,'chan'=4] {'chan'}, dimensions={0}, use_global_device_ids=true | all-gather | bytes 701440 | tf_op jit(solution)/shard_map/all_gather | solution.py:49
  285.3 19.7 %all_to_all.59 = f32[8,128,137]{1,2,0:T(8,128)S(1)} all-to-all(f32[8,128,137]{1,2,0:T(8,128)S(1)} %copy.195), channel_id=1, replica_groups=mesh['obs'=8,'chan'=4] {'obs'}, dimensions={0} | all-to-all | bytes 1122304 | tf_op jit(solution)/shard_map/all_to_all | solution.py:53
  306.4 1.7 reshape.237
  308.1 2.2 dot_general.218
  313.3 19.4 %psum.75 = f32[]{:T(128)} all-reduce(f32[]{:T(128)} %get-tuple-element.16), channel_id=1, replica_groups=mesh['obs'=8,'chan'=4] {'obs'}, use_global_device_ids=true, to_apply=%region_16.17 | all-reduce | flops 1 | bytes 8 | tf_op jit(solution)/shard_map/psum | solution.py:108
  334.8 18.1 %psum.76 = f32[]{:T(128)} all-reduce(f32[]{:T(128)} %get-tuple-element.6), channel_id=1, replica_groups=mesh['obs'=8,'chan'=4] {'obs'}, use_global_device_ids=true, to_apply=%region_18.19 | all-reduce | flops 1 | bytes 8 | tf_op jit(solution)/shard_map/psum | solution.py:81
  356.3 2.3 reshape.239
  359.5 12.8 %all_to_all.60 = bf16[8,128,137]{1,2,0:T(8,128)(2,1)} all-to-all(bf16[8,128,137]{1,2,0:T(8,128)(2,1)} %copy.201), channel_id=1, replica_groups=mesh['obs'=8,'chan'=4] {'obs'}, dimensions={0} | all-to-all | bytes 561152 | tf_op jit(solution)/shard_map/all_to_all | solution.py:92
  378.9 7.2 %all_gather.26 = f32[4,2,128,137]{2,1,3,0:T(2,128)S(1)} all-gather(f32[1,2,128,137]{2,1,3,0:T(2,128)} %all_gather_reshape.22), channel_id=1, replica_groups=mesh['obs'=8,'chan'=4] {'chan'}, dimensions={0}, use_global_device_ids=true | all-gather | bytes 701440 | tf_op jit(solution)/shard_map/all_gather | solution.py:49
  389.7 20.4 %all_to_all.61 = f32[8,128,137]{1,2,0:T(8,128)} all-to-all(f32[8,128,137]{1,2,0:T(8,128)S(1)} %copy.205), channel_id=1, replica_groups=mesh['obs'=8,'chan'=4] {'obs'}, dimensions={0} | all-to-all | bytes 1122304 | tf_op jit(solution)/shard_map/all_to_all | solution.py:53
  410.2 2.4 copy.206
  412.6 1.7 reshape.242
  414.3 2.2 dot_general.230
  416.4 1.6 copy.207
  419.5 19.4 %psum.77 = f32[]{:T(128)} all-reduce(f32[]{:T(128)} %get-tuple-element.18), channel_id=1, replica_groups=mesh['obs'=8,'chan'=4] {'obs'}, use_global_device_ids=true, to_apply=%region_21.22 | all-reduce | flops 1 | bytes 8 | tf_op jit(solution)/shard_map/psum | solution.py:108
  441.9 18.0 %psum.78 = f32[]{:T(128)} all-reduce(f32[]{:T(128)} %get-tuple-element.4), channel_id=1, replica_groups=mesh['obs'=8,'chan'=4] {'obs'}, use_global_device_ids=true, to_apply=%region_23.24 | all-reduce | flops 1 | bytes 8 | tf_op jit(solution)/shard_map/psum | solution.py:81
  464.0 2.0 reshape.244
  466.1 2.0 copy.211
  468.0 12.8 %all_to_all.62 = bf16[8,128,137]{1,2,0:T(8,128)(2,1)} all-to-all(bf16[8,128,137]{1,2,0:T(8,128)(2,1)} %copy.211), channel_id=1, replica_groups=mesh['obs'=8,'chan'=4] {'obs'}, dimensions={0} | all-to-all | bytes 561152 | tf_op jit(solution)/shard_map/all_to_all | solution.py:92
  480.9 2.0 copy.212
  482.8 2.4 reshape.245
  490.2 7.2 %all_gather.27 = f32[4,2,128,137]{2,1,3,0:T(2,128)S(1)} all-gather(f32[1,2,128,137]{2,1,3,0:T(2,128)S(1)} %all_gather_reshape.23), channel_id=1, replica_groups=mesh['obs'=8,'chan'=4] {'chan'}, dimensions={0}, use_global_device_ids=true | all-gather | bytes 701440 | tf_op jit(solution)/shard_map/all_gather | solution.py:49
  499.5 19.7 %all_to_all.63 = f32[8,128,137]{1,2,0:T(8,128)S(1)} all-to-all(f32[8,128,137]{1,2,0:T(8,128)S(1)} %copy.215), channel_id=1, replica_groups=mesh['obs'=8,'chan'=4] {'obs'}, dimensions={0} | all-to-all | bytes 1122304 | tf_op jit(solution)/shard_map/all_to_all | solution.py:53
  523.1 19.4 %psum.79 = f32[]{:T(128)} all-reduce(f32[]{:T(128)} %get-tuple-element.20), channel_id=1, replica_groups=mesh['obs'=8,'chan'=4] {'obs'}, use_global_device_ids=true, to_apply=%region_26.27 | all-reduce | flops 1 | bytes 8 | tf_op jit(solution)/shard_map/psum | solution.py:108
  (207 shorter events, 89.5 us)
Async XLA Ops:
  0.6 41.0 %copy-start = (f32[137,137]{1,0:T(8,128)S(1)}, f32[137,137]{1,0:T(8,128)}, u32[]{:S(2)}) copy-start(f32[137,137]{1,0:T(8,128)} %param.11) | copy-start | bytes 225232
  2.0 72.9 %copy-start.8 = (s32[2]{0:T(128)}, s32[2]{0:T(128)S(1)}, u32[]{:S(2)}) copy-start(s32[2]{0:T(128)S(1)} %and_select_fusion) | copy-start | bytes 28
  2.0 63.3 %copy-start.14 = (f32[256]{0:T(256)}, f32[256]{0:T(256)S(1)}, u32[]{:S(2)}) copy-start(f32[256]{0:T(256)S(1)} %compare_convert_fusion.1) | copy-start | bytes 3076
  14.5 8.4 %copy-start.20 = (u32[32]{0:T(128)S(1)}, u32[32]{0:T(128)}, u32[]{:S(2)}) copy-start(u32[32]{0:T(128)} %constant.47) | copy-start | bytes 388
  14.6 9.6 %copy-start.19 = (s32[2]{0:T(128)S(1)}, s32[2]{0:T(128)}, u32[]{:S(2)}) copy-start(s32[2]{0:T(128)} %param.10) | copy-start | bytes 28
  17.1 22.8 %all-to-all-start = ((f32[8,128,137]{1,2,0:T(8,128)}), f32[8,128,137]{1,2,0:T(8,128)S(1)}, u32[]{:S(2)}, u32[]{:S(2)}) async-start(f32[8,128,137]{1,2,0:T(8,128)} %copy.163), calls=%async_computation | async-start | bytes 1179648 | tf_op jit(solution)/shard_map/all_to_all | solution.py:53
  39.8 2.9 copy-start.11
  39.9 3.8 copy-start.17
  44.0 20.7 %copy-start.1 = (bf16[256,32,137]{0,1,2:T(8,128)(2,1)S(1)}, bf16[256,32,137]{0,1,2:T(8,128)(2,1)}, u32[]{:S(2)}) copy-start(bf16[256,32,137]{0,1,2:T(8,128)(2,1)} %param.6) | copy-start | bytes 6733828
  60.4 4.9 copy-start.5
  76.4 20.2 %all-to-all-start.2 = ((f32[8,128,137]{1,2,0:T(8,128)}), f32[8,128,137]{1,2,0:T(8,128)S(1)}, u32[]{:S(2)}, u32[]{:S(2)}) async-start(f32[8,128,137]{1,2,0:T(8,128)} %copy.170), calls=%async_computation.2 | async-start | bytes 1179648 | tf_op jit(solution)/shard_map/all_to_all | solution.py:53
  97.9 5.5 %copy-start.12 = (f32[2,8]{1,0:T(2,128)S(1)}, f32[2,8]{1,0:T(2,128)}, u32[]{:S(2)}) copy-start(f32[2,8]{1,0:T(2,128)} %copy-done.11) | copy-start | bytes 196
  101.8 45.3 %copy-start.18 = (bf16[2,8]{1,0:T(2,128)(2,1)S(1)}, bf16[2,8]{1,0:T(2,128)(2,1)}, u32[]{:S(2)}) copy-start(bf16[2,8]{1,0:T(2,128)(2,1)} %copy-done.17) | copy-start | bytes 100
  146.7 19.9 %copy-start.9 = (s32[2]{0:T(128)S(1)}, s32[2]{0:T(128)}, u32[]{:S(2)}) copy-start(s32[2]{0:T(128)} %copy-done.8) | copy-start | bytes 28
  164.1 4.9 copy-start.15
  232.7 20.5 %copy-start.3 = (f32[2,128,137]{1,2,0:T(8,128)}, f32[2,128,137]{1,2,0:T(8,128)S(1)}, u32[]{:S(2)}) copy-start(f32[2,128,137]{1,2,0:T(8,128)S(1)} %get-tuple-element.9) | copy-start | bytes 420868
  308.1 26.1 %copy-start.4 = (f32[2,128,137]{1,2,0:T(8,128)S(1)}, f32[2,128,137]{1,2,0:T(8,128)}, u32[]{:S(2)}) copy-start(f32[2,128,137]{1,2,0:T(8,128)} %copy-done.3) | copy-start | bytes 420868
  334.8 20.4 %copy-start.2 = (f32[2,128,137]{1,2,0:T(8,128)}, f32[2,128,137]{1,2,0:T(8,128)S(1)}, u32[]{:S(2)}) copy-start(f32[2,128,137]{1,2,0:T(8,128)S(1)} %get-tuple-element.7) | copy-start | bytes 420868
  372.3 4.9 copy-start.6
  480.9 8.3 %copy-start.7 = (f32[32,256]{1,0:T(8,128)S(1)}, f32[32,256]{1,0:T(8,128)}, u32[]{:S(2)}) copy-start(f32[32,256]{1,0:T(8,128)} %param.8) | copy-start | bytes 98308
  480.9 8.3 %copy-start.16 = (f32[256]{0:T(256)S(1)}, f32[256]{0:T(256)}, u32[]{:S(2)}) copy-start(f32[256]{0:T(256)} %copy-done.14) | copy-start | bytes 3076
  490.2 8.7 %copy-start.10 = (s32[2]{0:T(128)S(1)}, s32[2]{0:T(128)}, u32[]{:S(2)}) copy-start(s32[2]{0:T(128)} %copy-done.8) | copy-start | bytes 28
  519.5 2.1 copy-start.13
